TPU v7x, 32 devices: a whole 2x2x4 slice. The times are simulated.
32 devices in a mesh: groups: 2 (over x), ep: 16 (over z, y, core).
Axes of the slice: x: 2, y: 2, z: 4, core: 2. Of those that a mesh axis runs over, the one named last changes fastest.
Arguments:
- tokens: bfloat16 [256, 7168], P(('groups', 'ep')), parts along dimension 0, may hold values from -6 to 6
- experts: int32 [256, 8], P(('groups', 'ep')), parts along dimension 0, may hold values from 0 to 15, as said below
- gate_fixed: int32 [256, 8], P(('groups', 'ep')), parts along dimension 0, may hold values from 1 to 65535
- home_slot: int32 [256], P(('groups', 'ep')), parts along dimension 0, may hold values from 0 to 7, as said below
- bias: float32 [16], replicated, may hold values from -0.5 to 0.5
- w_gate: bfloat16 [7168, 32768], P(None, 'ep'), may hold values from -0.0625 to 0.0625
- w_up: bfloat16 [7168, 32768], P(None, 'ep'), may hold values from -0.0625 to 0.0625
- w_down: bfloat16 [32768, 7168], P('ep'), may hold values from -0.125 to 0.125
Outputs:
- moe_out: bfloat16 [256, 7168], P(('groups', 'ep')), parts along dimension 0
- bias_next: float32 [32], P('groups'), parts along dimension 0
There are 2 independent parts, one for each index of `groups`. A program takes and returns all parts, laid end to end along the dimension named above; an argument that names none is the same for every part. Nothing has to cross between parts.
Inputs may be any that keep to these rules, and one draw needn't show every extreme that they name: Each token names 8 different experts; among the tokens of one device no expert is named more than 6 times, and some device reaches that bound. `home_slot`: within each device's block of 8 tokens every value appears exactly once.
All inputs are finite; a program needn't handle non-finite values.
Results may differ from a plain program's by a relative error of at most 0.008.
Values may be sent and summed in bfloat16 or wider, within the bound.
A program may use at most 128 MiB of HBM per device.

v0:
```python
import functools
import math

import jax
import jax.numpy as jnp
from jax import lax
from jax.experimental import pallas as pl
from jax.experimental.pallas import tpu as pltpu
from jax.sharding import PartitionSpec as P

ROUTED_SCALE = 2.5


def expert_rows(row_block, w_gate, w_up, w_down):
    gate_part = jnp.dot(row_block, w_gate, preferred_element_type=jnp.float32)
    up_part = jnp.dot(row_block, w_up, preferred_element_type=jnp.float32)
    hidden = (jax.nn.silu(gate_part) * up_part).astype(jnp.bfloat16)
    return jnp.dot(hidden, w_down, preferred_element_type=jnp.float32).astype(jnp.bfloat16)


def general(tokens, experts, gate_fixed, home_slot, bias, w_gate, w_up, w_down):
    tok_rows, model_width = tokens.shape
    top_count = experts.shape[1]
    expert_count = bias.shape[0]
    device_count = lax.axis_size("ep")
    shards = device_count // expert_count
    capacity = max(
        2, min(tok_rows, (3 * tok_rows * top_count + 2 * expert_count - 1) // (2 * expert_count))
    )
    pair_count = tok_rows * top_count
    flat_ids = experts.reshape(pair_count)
    hit_table = (flat_ids[:, None] == jnp.arange(expert_count, dtype=jnp.int32)[None, :]).astype(
        jnp.int32
    )
    earlier = jnp.cumsum(hit_table, axis=0) - hit_table
    slot_rank = jnp.sum(earlier * hit_table, axis=1)
    dest_row = flat_ids * capacity + slot_rank
    pair_source = jnp.arange(pair_count, dtype=jnp.int32) // top_count
    fixed_gate = gate_fixed.astype(jnp.float32)
    gate_share = ROUTED_SCALE * fixed_gate / jnp.sum(fixed_gate, axis=1, keepdims=True)
    outgoing = (
        jnp.zeros((expert_count * capacity, model_width), jnp.bfloat16)
        .at[dest_row]
        .set(tokens[pair_source])
    )
    outgoing = jnp.broadcast_to(
        outgoing.reshape(expert_count, 1, capacity, model_width),
        (expert_count, shards, capacity, model_width),
    )
    outgoing = outgoing.reshape(device_count, capacity, model_width)
    used_slots = jnp.zeros((expert_count * capacity,), jnp.bfloat16).at[dest_row].set(1.0)
    used_slots = jnp.broadcast_to(
        used_slots.reshape(expert_count, 1, capacity), (expert_count, shards, capacity)
    ).reshape(device_count, capacity)
    payload = (outgoing,)
    pieces = (lax.all_to_all(payload[0], "ep", split_axis=0, concat_axis=0, tiled=True),)
    sources, slot_count, _ = pieces[0].shape
    results = expert_rows(
        pieces[0].reshape(sources * slot_count, model_width), w_gate, w_up, w_down
    )
    answer = lax.all_to_all(
        results.reshape(sources, slot_count, model_width),
        "ep",
        split_axis=0,
        concat_axis=0,
        tiled=True,
    )
    landed = (answer,) + tuple(pieces[1:])
    returned = landed[0]
    loads = lax.psum(jnp.sum(hit_table, axis=0), "ep")
    summed = jnp.sum(
        returned.reshape(expert_count, shards, capacity, model_width), axis=1, dtype=jnp.float32
    )
    summed = summed.reshape(expert_count * capacity, model_width)
    picked = summed[dest_row].reshape(tok_rows, top_count, model_width)
    combined = jnp.sum(picked * gate_share[:, :, None], axis=1).astype(jnp.bfloat16)
    placer = (home_slot[None, :] == jnp.arange(tok_rows, dtype=jnp.int32)[:, None]).astype(
        jnp.bfloat16
    )
    placed = jnp.dot(placer, combined, preferred_element_type=jnp.float32).astype(jnp.bfloat16)
    average = tok_rows * device_count * top_count / expert_count
    bias_next = bias + 2.0 / math.sqrt(average) * (average - loads.astype(jnp.float32))
    return (placed, bias_next)


LANES = 128
HID_COLS = 256
OUT_COLS = 1024
GU_SLOTS = 6
DN_SLOTS = 2
LAG_Y, LAG_Z, LAG_OUT = 1, 2, 3


def flip(z, m, nz):
    bit = 1
    while bit < nz:
        if m & bit:
            z = z + bit - 2 * bit * ((z // bit) % 2)
        bit *= 2
    return z


def moe_kernel(
    nz, experts_total, average,
    tokens_hbm, experts_hbm, gates_hbm, home_hbm, bias_hbm, wg_hbm, wu_hbm, wd_hbm,
    out_ref, bias_out,
    tok_v, exp_v, gate_v, home_v, bias_v, gath, x_v, gu_v, dn_v, hid_v, share_v,
    p_v, r1_v, s1_v, r2_v, s2_v, r3_v,
    in_sem, gu_sem, dn_sem, zs, zr, ys, yr, cs, cr,
    s1s, s1r, s2s, s2r, s3s, s3r,
):
    rows, depth = tok_v.shape
    top = exp_v.shape[1]
    ff = hid_v.shape[1]
    gu_count = ff // HID_COLS
    out_count = depth // OUT_COLS
    blocks = 4 * nz
    me = lax.axis_index("ep")
    core = me % 2
    y = (me // 2) % 2
    z = me // 4
    other_core = z * 4 + y * 2 + (1 - core)
    other_y = z * 4 + (1 - y) * 2 + core

    def z_peer(m):
        return flip(z, m, nz) * 4 + y * 2 + core

    def slot_of(zz, yy, cc):
        return (cc * 2 + yy) * nz + zz

    small = [
        pltpu.make_async_copy(tokens_hbm, tok_v, in_sem.at[0]),
        pltpu.make_async_copy(experts_hbm, exp_v, in_sem.at[1]),
        pltpu.make_async_copy(gates_hbm, gate_v, in_sem.at[2]),
        pltpu.make_async_copy(home_hbm, home_v, in_sem.at[3]),
        pltpu.make_async_copy(bias_hbm, bias_v, in_sem.at[4]),
    ]
    for copy in small:
        copy.start()

    def gu_copies(i):
        slot = lax.rem(i, GU_SLOTS)
        cols = pl.ds(pl.multiple_of(i * HID_COLS, HID_COLS), HID_COLS)
        return [
            pltpu.make_async_copy(w.at[:, cols], gu_v.at[slot, k], gu_sem.at[i, k])
            for k, w in enumerate((wg_hbm, wu_hbm))
        ]

    def dn_copy(j):
        slot = lax.rem(j, DN_SLOTS)
        cols = pl.ds(pl.multiple_of(j * OUT_COLS, OUT_COLS), OUT_COLS)
        return pltpu.make_async_copy(wd_hbm.at[:, cols], dn_v.at[slot], dn_sem.at[j])

    def start_gu(i, carry):
        for copy in gu_copies(i):
            copy.start()
        return carry

    def start_dn(j, carry):
        dn_copy(j).start()
        return carry

    lax.fori_loop(0, min(GU_SLOTS, gu_count), start_gu, 0)
    lax.fori_loop(0, min(DN_SLOTS, out_count), start_dn, 0)

    barrier = pltpu.get_barrier_semaphore()
    peers = [other_core, other_y] + [z_peer(m) for m in range(1, nz)]
    for peer in peers:
        pl.semaphore_signal(
            barrier, inc=1, device_id={"ep": peer}, device_id_type=pl.DeviceIdType.MESH
        )

    for copy in small:
        copy.wait()

    lane = lax.broadcasted_iota(jnp.int32, (rows, LANES), 1)
    lane_expert = lane % experts_total
    part = lane // experts_total
    gates = gate_v[...].astype(jnp.float32)
    shares = ROUTED_SCALE * gates / jnp.sum(gates, axis=1, keepdims=True)
    ids = exp_v[...]
    table = jnp.zeros((rows, LANES), jnp.float32)
    hits = jnp.zeros((rows, LANES), jnp.float32)
    for k in range(top):
        match = ids[:, k : k + 1] == lane_expert
        table += jnp.where(match, shares[:, k : k + 1], 0.0)
        hits += jnp.where(match, 1.0, 0.0)
    home = home_v[...]
    row_id = lax.broadcasted_iota(jnp.int32, (rows, 1), 0)
    moved = jnp.zeros((rows, depth), jnp.float32)
    moved_table = jnp.zeros((rows, LANES), jnp.float32)
    moved_hits = jnp.zeros((rows, LANES), jnp.float32)
    token_rows = tok_v[...].astype(jnp.float32)
    for t in range(rows):
        here = row_id == home[:, t : t + 1]
        moved = jnp.where(here, token_rows[t : t + 1, :], moved)
        moved_table = jnp.where(here, table[t : t + 1, :], moved_table)
        moved_hits = jnp.where(here, hits[t : t + 1, :], moved_hits)
    high = moved_table.astype(jnp.bfloat16).astype(jnp.float32)
    rest = moved_table - high
    middle = rest.astype(jnp.bfloat16).astype(jnp.float32)
    low = rest - middle
    packed = jnp.where(
        part == 0,
        moved_hits,
        jnp.where(part == 1, high, jnp.where(part == 2, middle, jnp.where(part == 3, low, 0.0))),
    )
    mine = slot_of(z, y, core)
    gath[mine, :, :depth] = moved.astype(jnp.bfloat16)
    gath[mine, :, depth:] = packed.astype(jnp.bfloat16)

    pl.semaphore_wait(barrier, len(peers))

    def send(slot, peer, ssem, rsem):
        return pltpu.make_async_remote_copy(
            src_ref=gath.at[slot],
            dst_ref=gath.at[slot],
            send_sem=ssem,
            recv_sem=rsem,
            device_id={"ep": peer},
            device_id_type=pl.DeviceIdType.MESH,
        )

    z_order = list(range(nz - 1, 0, -1))
    z_sends = {m: send(mine, z_peer(m), zs.at[m], zr.at[m]) for m in z_order}
    y_sends = {0: send(mine, other_y, ys.at[0], yr.at[0])}
    c_sends = {0: send(mine, other_core, cs.at[0], cr.at[0])}
    for m in z_order:
        z_sends[m].start()
    y_sends[0].start()
    c_sends[0].start()
    for m in z_order:
        slot = slot_of(flip(z, m, nz), y, core)
        y_sends[m] = send(slot, other_y, ys.at[m], yr.at[m])
        c_sends[m] = send(slot, other_core, cs.at[m], cr.at[m])
    for m in range(nz):
        slot = slot_of(flip(z, m, nz), 1 - y, core)
        c_sends[nz + m] = send(slot, other_core, cs.at[nz + m], cr.at[nz + m])
    y_sends[0].wait_recv()
    c_sends[nz].start()
    for m in z_order:
        z_sends[m].wait_recv()
        y_sends[m].start()
        c_sends[m].start()
    for m in z_order:
        y_sends[m].wait_recv()
        c_sends[nz + m].start()
    for k in range(2 * nz):
        c_sends[k].wait_recv()

    def spread(b, carry):
        pair = jnp.concatenate(
            [
                gath[2 * b, :, :depth].astype(jnp.float32),
                gath[2 * b + 1, :, :depth].astype(jnp.float32),
            ],
            axis=0,
        )
        x_v[pl.ds(pl.multiple_of(b * 2 * rows, 2 * rows), 2 * rows), :] = pair.astype(jnp.bfloat16)
        return carry

    lax.fori_loop(0, blocks // 2, spread, 0)
    tables = gath[:, :, depth:].astype(jnp.float32).reshape(blocks * rows, LANES)
    lane = lax.broadcasted_iota(jnp.int32, (blocks * rows, LANES), 1)
    wanted = (lane % experts_total == me) & (lane // experts_total > 0)
    share = jnp.sum(jnp.where(wanted, tables, 0.0), axis=1, keepdims=True)
    share_v[...] = jnp.broadcast_to(share, share_v.shape)
    load = jnp.sum(tables, axis=0, keepdims=True)[:, :experts_total]
    bias_out[...] = bias_v[...] + 2.0 / math.sqrt(average) * (average - load)

    def gu_step(i, carry):
        for copy in gu_copies(i):
            copy.wait()
        slot = lax.rem(i, GU_SLOTS)
        x = x_v[...]
        gate = jnp.dot(x, gu_v[slot, 0], preferred_element_type=jnp.float32)
        up = jnp.dot(x, gu_v[slot, 1], preferred_element_type=jnp.float32)
        cols = pl.ds(pl.multiple_of(i * HID_COLS, HID_COLS), HID_COLS)
        hid_v[:, cols] = (gate / (1.0 + jnp.exp(-gate)) * up).astype(jnp.bfloat16)

        @pl.when(i + GU_SLOTS < gu_count)
        def _():
            start_gu(i + GU_SLOTS, 0)

        return carry

    lax.fori_loop(0, gu_count, gu_step, 0)

    def remote(src, dst, ssem, rsem, peer):
        return pltpu.make_async_remote_copy(
            src_ref=src,
            dst_ref=dst,
            send_sem=ssem,
            recv_sem=rsem,
            device_id={"ep": peer},
            device_id_type=pl.DeviceIdType.MESH,
        )

    def send_core(j):
        return remote(p_v.at[j, 1 - core], r1_v.at[j], s1s.at[j], s1r.at[j], other_core)

    def send_y(j):
        return remote(s1_v.at[j, 1 - y], r2_v.at[j], s2s.at[j], s2r.at[j], other_y)

    def send_z(j, m):
        return remote(
            s2_v.at[j, flip(z, m, nz)], r3_v.at[j, m - 1], s3s.at[j, m], s3r.at[j, m], z_peer(m)
        )

    half = blocks * rows // 2
    quarter = half // 2

    def step(j, carry):
        @pl.when(j < out_count)
        def _():
            dn_copy(j).wait()
            slot = lax.rem(j, DN_SLOTS)
            value = jnp.dot(hid_v[...], dn_v[slot], preferred_element_type=jnp.float32)
            value = (value * share_v[:, :1]).astype(jnp.bfloat16)
            p_v[j, 0] = value[:half]
            p_v[j, 1] = value[half:]
            send_core(j).start()

            @pl.when(j + DN_SLOTS < out_count)
            def _():
                start_dn(j + DN_SLOTS, 0)

        @pl.when((j >= LAG_Y) & (j < out_count + LAG_Y))
        def _():
            i = j - LAG_Y
            send_core(i).wait_recv()
            value = p_v[i, core].astype(jnp.float32) + r1_v[i].astype(jnp.float32)
            value = value.astype(jnp.bfloat16)
            s1_v[i, 0] = value[:quarter]
            s1_v[i, 1] = value[quarter:]
            send_y(i).start()

        @pl.when((j >= LAG_Z) & (j < out_count + LAG_Z))
        def _():
            i = j - LAG_Z
            send_y(i).wait_recv()
            value = s1_v[i, y].astype(jnp.float32) + r2_v[i].astype(jnp.float32)
            s2_v[i] = value.reshape(nz, rows, OUT_COLS).astype(jnp.bfloat16)
            for m in z_order:
                send_z(i, m).start()

        @pl.when(j >= LAG_OUT)
        def _():
            i = j - LAG_OUT
            value = s2_v[i, z].astype(jnp.float32)
            for m in z_order:
                send_z(i, m).wait_recv()
            for m in z_order:
                value += r3_v[i, m - 1].astype(jnp.float32)
            cols = pl.ds(pl.multiple_of(i * OUT_COLS, OUT_COLS), OUT_COLS)
            out_ref[:, cols] = value.astype(jnp.bfloat16)

        return carry

    lax.fori_loop(0, out_count + LAG_OUT, step, 0)

    for m in z_order:
        z_sends[m].wait_send()
    for m in range(nz):
        y_sends[m].wait_send()
    for k in range(2 * nz):
        c_sends[k].wait_send()

    def drain(j, carry):
        send_core(j).wait_send()
        send_y(j).wait_send()
        for m in z_order:
            send_z(j, m).wait_send()
        return carry

    lax.fori_loop(0, out_count, drain, 0)


def fits_kernel(tokens, experts, bias, w_gate, device_count):
    rows, depth = tokens.shape
    ff = w_gate.shape[1]
    nz = device_count // 4
    return (
        device_count == bias.shape[0]
        and device_count == 4 * nz
        and nz & (nz - 1) == 0
        and rows == 8
        and 4 * bias.shape[0] <= LANES
        and depth % OUT_COLS == 0
        and ff % HID_COLS == 0
        and GU_SLOTS * 4 * depth * HID_COLS
        + DN_SLOTS * 2 * ff * OUT_COLS
        + 21 * device_count * rows * depth // 2
        < 66600000
    )


def per_device(tokens, experts, gate_fixed, home_slot, bias, w_gate, w_up, w_down):
    device_count = lax.axis_size("ep")
    if not fits_kernel(tokens, experts, bias, w_gate, device_count):
        return general(tokens, experts, gate_fixed, home_slot, bias, w_gate, w_up, w_down)
    rows, depth = tokens.shape
    top = experts.shape[1]
    ff = w_gate.shape[1]
    expert_count = bias.shape[0]
    nz = device_count // 4
    total = device_count * rows
    out_count = depth // OUT_COLS
    average = rows * device_count * top / expert_count
    bf16 = jnp.bfloat16
    dma = pltpu.SemaphoreType.DMA
    anywhere = pl.BlockSpec(memory_space=pl.ANY)
    out, bias_next = pl.pallas_call(
        functools.partial(moe_kernel, nz, expert_count, average),
        out_shape=(
            jax.ShapeDtypeStruct((rows, depth), bf16),
            jax.ShapeDtypeStruct((1, expert_count), jnp.float32),
        ),
        in_specs=[anywhere] * 8,
        out_specs=(
            pl.BlockSpec(memory_space=pltpu.VMEM),
            pl.BlockSpec(memory_space=pltpu.VMEM),
        ),
        scratch_shapes=[
            pltpu.VMEM((rows, depth), bf16),
            pltpu.VMEM((rows, top), jnp.int32),
            pltpu.VMEM((rows, top), jnp.int32),
            pltpu.VMEM((1, rows), jnp.int32),
            pltpu.VMEM((1, expert_count), jnp.float32),
            pltpu.VMEM((device_count, rows, depth + LANES), bf16),
            pltpu.VMEM((total, depth), bf16),
            pltpu.VMEM((GU_SLOTS, 2, depth, HID_COLS), bf16),
            pltpu.VMEM((DN_SLOTS, ff, OUT_COLS), bf16),
            pltpu.VMEM((total, ff), bf16),
            pltpu.VMEM((total, LANES), jnp.float32),
            pltpu.VMEM((out_count, 2, total // 2, OUT_COLS), bf16),
            pltpu.VMEM((out_count, total // 2, OUT_COLS), bf16),
            pltpu.VMEM((out_count, 2, total // 4, OUT_COLS), bf16),
            pltpu.VMEM((out_count, total // 4, OUT_COLS), bf16),
            pltpu.VMEM((out_count, nz, rows, OUT_COLS), bf16),
            pltpu.VMEM((out_count, nz - 1, rows, OUT_COLS), bf16),
            dma((5,)),
            dma((ff // HID_COLS, 2)),
            dma((out_count,)),
            dma((nz,)),
            dma((nz,)),
            dma((nz,)),
            dma((nz,)),
            dma((2 * nz,)),
            dma((2 * nz,)),
            dma((out_count,)),
            dma((out_count,)),
            dma((out_count,)),
            dma((out_count,)),
            dma((out_count, nz)),
            dma((out_count, nz)),
        ],
        compiler_params=pltpu.CompilerParams(
            collective_id=0, has_side_effects=True, vmem_limit_bytes=67043328
        ),
    )(
        tokens,
        experts,
        gate_fixed,
        home_slot.reshape(1, rows),
        bias.reshape(1, expert_count),
        w_gate,
        w_up,
        w_down,
    )
    return out, bias_next.reshape(expert_count)


def solution(mesh):
    placed = (
        P(("groups", "ep"), None),
        P(("groups", "ep"), None),
        P(("groups", "ep"), None),
        P(("groups", "ep")),
        P(),
        P(None, "ep"),
        P(None, "ep"),
        P("ep", None),
    )
    return jax.shard_map(
        per_device,
        mesh=mesh,
        in_specs=placed,
        out_specs=(P(("groups", "ep"), None), P("groups")),
        check_vma=False,
    )
```

profile of v0, /device:TPU:0, one launch (start us, length us, event | category | flops | bytes accessed | tf_op | source)
XLA Modules:
  0.0 62.6 jit_solution(14065468148044543530)
XLA Ops:
  0.6 59.3 %shard_map.95 = (bf16[8,7168]{1,0:T(8,128)(2,1)}, f32[1,16]{1,0:T(1,128)}) custom-call(bf16[8,7168]{1,0:T(8,128)(2,1)} %tokens_hbm.1, s32[8,8]{1,0:T(8,128)} %experts_hbm.1, s32[8,8]{1,0:T(8,128)} %gates_hbm.1, s32[1,8]{1,0:T(1,128)} %bitcast.3, f32[1,16]{1,0:T(1,128)} %bitcast.4, bf16[7168,2048]{1,0:T(8,128)(2,1)} %wg_hbm.1, bf16[7168,2048]{1,0:T(8,128)(2,1)} %wu_hbm.1, ...), custom_call_target="tpu_custom_call" | custom-call | tf_op jit(solution)/shard_map/pallas_call | solution.py:413
  59.9 1.6 %copy.12 = bf16[8,7168]{1,0:T(8,128)(2,1)} copy(bf16[8,7168]{1,0:T(8,128)(2,1)} %get-tuple-element.8) | data formatting | bytes 229376
  61.5 1.1 %copy.13 = f32[16]{0:T(128)} copy(f32[16]{0:T(128)} %bitcast.5) | data formatting | bytes 128
where the time goes:
time: 62.7 us; the launch traced here: 62.6 us
  Pallas kernels  59.3 us (95%)
  local copies, waits for them, and re-layouts  2.66 us (4%)
  between operations  0.64 us (1%)
    pallas_call x1, Pallas kernels, per_device(): pl.pallas_call(functools.partial(moe_kernel, nz, expert_count, average),...  59.3 us
    unnamed x2, local copies, waits for them, and re-layouts  2.66 us

commit v1 on v0

v1 whole, which is shorter than its diff:
```python
import functools
import math

import jax
import jax.numpy as jnp
from jax import lax
from jax.experimental import pallas as pl
from jax.experimental.pallas import tpu as pltpu
from jax.sharding import PartitionSpec as P

ROUTED_SCALE = 2.5


def expert_rows(row_block, w_gate, w_up, w_down):
    gate_part = jnp.dot(row_block, w_gate, preferred_element_type=jnp.float32)
    up_part = jnp.dot(row_block, w_up, preferred_element_type=jnp.float32)
    hidden = (jax.nn.silu(gate_part) * up_part).astype(jnp.bfloat16)
    return jnp.dot(hidden, w_down, preferred_element_type=jnp.float32).astype(jnp.bfloat16)


def general(tokens, experts, gate_fixed, home_slot, bias, w_gate, w_up, w_down):
    tok_rows, model_width = tokens.shape
    top_count = experts.shape[1]
    expert_count = bias.shape[0]
    device_count = lax.axis_size("ep")
    shards = device_count // expert_count
    capacity = max(
        2, min(tok_rows, (3 * tok_rows * top_count + 2 * expert_count - 1) // (2 * expert_count))
    )
    pair_count = tok_rows * top_count
    flat_ids = experts.reshape(pair_count)
    hit_table = (flat_ids[:, None] == jnp.arange(expert_count, dtype=jnp.int32)[None, :]).astype(
        jnp.int32
    )
    earlier = jnp.cumsum(hit_table, axis=0) - hit_table
    slot_rank = jnp.sum(earlier * hit_table, axis=1)
    dest_row = flat_ids * capacity + slot_rank
    pair_source = jnp.arange(pair_count, dtype=jnp.int32) // top_count
    fixed_gate = gate_fixed.astype(jnp.float32)
    gate_share = ROUTED_SCALE * fixed_gate / jnp.sum(fixed_gate, axis=1, keepdims=True)
    outgoing = (
        jnp.zeros((expert_count * capacity, model_width), jnp.bfloat16)
        .at[dest_row]
        .set(tokens[pair_source])
    )
    outgoing = jnp.broadcast_to(
        outgoing.reshape(expert_count, 1, capacity, model_width),
        (expert_count, shards, capacity, model_width),
    )
    outgoing = outgoing.reshape(device_count, capacity, model_width)
    used_slots = jnp.zeros((expert_count * capacity,), jnp.bfloat16).at[dest_row].set(1.0)
    used_slots = jnp.broadcast_to(
        used_slots.reshape(expert_count, 1, capacity), (expert_count, shards, capacity)
    ).reshape(device_count, capacity)
    payload = (outgoing,)
    pieces = (lax.all_to_all(payload[0], "ep", split_axis=0, concat_axis=0, tiled=True),)
    sources, slot_count, _ = pieces[0].shape
    results = expert_rows(
        pieces[0].reshape(sources * slot_count, model_width), w_gate, w_up, w_down
    )
    answer = lax.all_to_all(
        results.reshape(sources, slot_count, model_width),
        "ep",
        split_axis=0,
        concat_axis=0,
        tiled=True,
    )
    landed = (answer,) + tuple(pieces[1:])
    returned = landed[0]
    loads = lax.psum(jnp.sum(hit_table, axis=0), "ep")
    summed = jnp.sum(
        returned.reshape(expert_count, shards, capacity, model_width), axis=1, dtype=jnp.float32
    )
    summed = summed.reshape(expert_count * capacity, model_width)
    picked = summed[dest_row].reshape(tok_rows, top_count, model_width)
    combined = jnp.sum(picked * gate_share[:, :, None], axis=1).astype(jnp.bfloat16)
    placer = (home_slot[None, :] == jnp.arange(tok_rows, dtype=jnp.int32)[:, None]).astype(
        jnp.bfloat16
    )
    placed = jnp.dot(placer, combined, preferred_element_type=jnp.float32).astype(jnp.bfloat16)
    average = tok_rows * device_count * top_count / expert_count
    bias_next = bias + 2.0 / math.sqrt(average) * (average - loads.astype(jnp.float32))
    return (placed, bias_next)


LANES = 128
GAT_COLS = 1024
OUT_COLS = 512
HID_COLS = 1024
SLOTS = 6
LAG_Y, LAG_C = 2, 3
LAG_1, LAG_2, LAG_3 = 2, 6, 12


def flip(z, m, nz):
    bit = 1
    while bit < nz:
        if m & bit:
            z = z + bit - 2 * bit * ((z // bit) % 2)
        bit *= 2
    return z


def moe_kernel(
    nz, experts_total, average,
    tokens_hbm, experts_hbm, gates_hbm, home_hbm, bias_hbm, wg_hbm, wu_hbm, wd_hbm,
    out_ref, bias_out,
    exp_v, gate_v, home_v, bias_v, gath, tab_v, x_v, w_v, acc_v, hid_v, share_v,
    p_v, r1_v, s1_v, r2_v, s2_v, r3_v,
    in_sem, gu_sem, dn_sem, zs, zr, ys, yr, cs, cr,
    s1s, s1r, s2s, s2r, s3s, s3r,
):
    rows, depth = tokens_hbm.shape
    top = exp_v.shape[1]
    ff = hid_v.shape[1]
    chunks = depth // GAT_COLS
    out_count = depth // OUT_COLS
    per_slot = ff // OUT_COLS
    blocks = 4 * nz
    side = 2 * nz
    me = lax.axis_index("ep")
    core = me % 2
    y = (me // 2) % 2
    z = me // 4
    other_core = z * 4 + y * 2 + (1 - core)
    other_y = z * 4 + (1 - y) * 2 + core

    def z_peer(m):
        return flip(z, m, nz) * 4 + y * 2 + core

    def slot_of(zz, yy, cc):
        return (cc * 2 + yy) * nz + zz

    def remote(src, dst, ssem, rsem, peer):
        return pltpu.make_async_remote_copy(
            src_ref=src,
            dst_ref=dst,
            send_sem=ssem,
            recv_sem=rsem,
            device_id={"ep": peer},
            device_id_type=pl.DeviceIdType.MESH,
        )

    mine = slot_of(z, y, core)
    token_copy = pltpu.make_async_copy(tokens_hbm, gath.at[mine], in_sem.at[0])
    small = [
        pltpu.make_async_copy(experts_hbm, exp_v, in_sem.at[1]),
        pltpu.make_async_copy(gates_hbm, gate_v, in_sem.at[2]),
        pltpu.make_async_copy(home_hbm, home_v, in_sem.at[3]),
        pltpu.make_async_copy(bias_hbm, bias_v, in_sem.at[4]),
    ]
    token_copy.start()
    for copy in small:
        copy.start()

    barrier = pltpu.get_barrier_semaphore()
    peers = [other_core, other_y] + [z_peer(m) for m in range(1, nz)]
    for peer in peers:
        pl.semaphore_signal(
            barrier, inc=1, device_id={"ep": peer}, device_id_type=pl.DeviceIdType.MESH
        )

    def gu_copies(g):
        slot = lax.rem(g, SLOTS)
        part = pl.ds(pl.multiple_of(g * GAT_COLS, GAT_COLS), GAT_COLS)
        return [
            pltpu.make_async_copy(w.at[part, :], w_v.at[slot, k], gu_sem.at[g, k])
            for k, w in enumerate((wg_hbm, wu_hbm))
        ]

    def dn_copies(j):
        slot = lax.rem(chunks + lax.div(j, per_slot), SLOTS)
        src = pl.ds(pl.multiple_of(j * OUT_COLS, OUT_COLS), OUT_COLS)
        dst = pl.ds(pl.multiple_of(lax.rem(j, per_slot) * OUT_COLS, OUT_COLS), OUT_COLS)
        return [
            pltpu.make_async_copy(
                wd_hbm.at[pl.ds(k * GAT_COLS, GAT_COLS), src],
                w_v.at[slot, k, :, dst],
                dn_sem.at[j, k],
            )
            for k in range(2)
        ]

    def start_gu(g, carry):
        for copy in gu_copies(g):
            copy.start()
        return carry

    def start_dn(j, carry):
        for copy in dn_copies(j):
            copy.start()
        return carry

    lax.fori_loop(0, min(SLOTS, chunks), start_gu, 0)

    def refill(g):
        @pl.when(g + SLOTS < chunks)
        def _():
            start_gu(g + SLOTS, 0)

        @pl.when(g + SLOTS >= chunks)
        def _():
            first = jnp.minimum((g + SLOTS - chunks) * per_slot, out_count)
            last = jnp.minimum(first + per_slot, out_count)
            lax.fori_loop(first, last, start_dn, 0)

    def cols_of(g):
        return pl.ds(pl.multiple_of(g * GAT_COLS, GAT_COLS), GAT_COLS)

    def send_z(g, m):
        ref = gath.at[mine, :, cols_of(g)]
        return remote(ref, ref, zs.at[g, m], zr.at[g, m], z_peer(m))

    def send_y(g, m):
        ref = gath.at[slot_of(flip(z, m, nz), y, core), :, cols_of(g)]
        return remote(ref, ref, ys.at[g, m], yr.at[g, m], other_y)

    def send_own_y():
        ref = gath.at[mine]
        return remote(ref, ref, ys.at[0, 0], yr.at[0, 0], other_y)

    def send_c(g):
        ref = gath.at[pl.ds(core * side, side), :, cols_of(g)]
        return remote(ref, ref, cs.at[g], cr.at[g], other_core)

    def table_z(m):
        ref = tab_v.at[mine]
        return remote(ref, ref, zs.at[chunks, m], zr.at[chunks, m], z_peer(m))

    def table_y():
        ref = tab_v.at[pl.ds(slot_of(0, y, core), nz)]
        return remote(ref, ref, ys.at[chunks, 0], yr.at[chunks, 0], other_y)

    def table_c():
        ref = tab_v.at[pl.ds(core * side, side)]
        return remote(ref, ref, cs.at[chunks], cr.at[chunks], other_core)

    z_order = list(range(nz - 1, 0, -1))

    token_copy.wait()
    pl.semaphore_wait(barrier, len(peers))

    send_own_y().start()

    def first_sends(g, carry):
        for m in z_order:
            send_z(g, m).start()
        return carry

    lax.fori_loop(0, chunks, first_sends, 0)

    for copy in small:
        copy.wait()
    lane = lax.broadcasted_iota(jnp.int32, (rows, LANES), 1)
    lane_expert = lane % experts_total
    part = lane // experts_total
    gates = gate_v[...].astype(jnp.float32)
    shares = ROUTED_SCALE * gates / jnp.sum(gates, axis=1, keepdims=True)
    ids = exp_v[...]
    table = jnp.zeros((rows, LANES), jnp.float32)
    hits = jnp.zeros((rows, LANES), jnp.float32)
    for k in range(top):
        match = ids[:, k : k + 1] == lane_expert
        table += jnp.where(match, shares[:, k : k + 1], 0.0)
        hits += jnp.where(match, 1.0, 0.0)
    high = table.astype(jnp.bfloat16).astype(jnp.float32)
    rest = table - high
    middle = rest.astype(jnp.bfloat16).astype(jnp.float32)
    low = rest - middle
    packed = jnp.where(
        part == 0,
        hits,
        jnp.where(part == 1, high, jnp.where(part == 2, middle, jnp.where(part == 3, low, 0.0))),
    )
    tab_v[mine] = packed.astype(jnp.bfloat16)
    for m in z_order:
        table_z(m).start()
    acc_v[...] = jnp.zeros_like(acc_v)

    def spread(b, g):
        pair = jnp.concatenate(
            [
                gath[2 * b, :, cols_of(g)].astype(jnp.float32),
                gath[2 * b + 1, :, cols_of(g)].astype(jnp.float32),
            ],
            axis=0,
        )
        x_v[pl.ds(pl.multiple_of(b * 2 * rows, 2 * rows), 2 * rows), :] = pair.astype(jnp.bfloat16)
        return g

    def stage_z(g):
        for m in range(1, nz):
            send_z(g, m).wait_recv()
            send_y(g, m).start()

    def stage_y(g):
        for m in range(1, nz):
            send_y(g, m).wait_recv()
        send_c(g).start()

    def stage_c(g):
        send_c(g).wait_recv()
        lax.fori_loop(0, blocks // 2, spread, g)
        for copy in gu_copies(g):
            copy.wait()

    def products(g, n):
        slot = lax.rem(g, SLOTS)
        cols = pl.ds(pl.multiple_of(n * HID_COLS, HID_COLS), HID_COLS)
        x = x_v[...]
        gate = jnp.dot(x, w_v[slot, 0, :, cols], preferred_element_type=jnp.float32)
        up = jnp.dot(x, w_v[slot, 1, :, cols], preferred_element_type=jnp.float32)
        return acc_v[0, :, cols] + gate, acc_v[1, :, cols] + up, cols

    def gather_step(i, carry):
        @pl.when(i < chunks)
        def _():
            stage_z(i)

        @pl.when(i == 0)
        def _():
            for m in z_order:
                table_z(m).wait_recv()
            table_y().start()

        @pl.when(i == LAG_Y)
        def _():
            send_own_y().wait_recv()
            table_y().wait_recv()
            table_c().start()

        @pl.when((i >= LAG_Y) & (i < chunks + LAG_Y))
        def _():
            stage_y(i - LAG_Y)

        @pl.when(i >= LAG_C)
        def _():
            g = i - LAG_C
            stage_c(g)

            def body(n, carry):
                gate, up, cols = products(g, n)
                acc_v[0, :, cols] = gate
                acc_v[1, :, cols] = up
                return carry

            lax.fori_loop(0, ff // HID_COLS, body, 0)
            refill(g)

        return carry

    lax.fori_loop(0, chunks + LAG_C - 1, gather_step, 0)

    table_c().wait_recv()
    tables = tab_v[...].astype(jnp.float32).reshape(blocks * rows, LANES)
    lane = lax.broadcasted_iota(jnp.int32, (blocks * rows, LANES), 1)
    wanted = (lane % experts_total == me) & (lane // experts_total > 0)
    share = jnp.sum(jnp.where(wanted, tables, 0.0), axis=1, keepdims=True)
    share_v[...] = jnp.broadcast_to(share, share_v.shape)
    load = jnp.sum(tables, axis=0, keepdims=True)[:, :experts_total]
    bias_out[...] = bias_v[...] + 2.0 / math.sqrt(average) * (average - load)

    stage_c(chunks - 1)

    def last_body(n, carry):
        gate, up, cols = products(chunks - 1, n)
        hid_v[:, cols] = (gate / (1.0 + jnp.exp(-gate)) * up).astype(jnp.bfloat16)
        return carry

    lax.fori_loop(0, ff // HID_COLS, last_body, 0)
    refill(chunks - 1)

    def send_1(j):
        return remote(p_v.at[j, 1 - core], r1_v.at[j], s1s.at[j], s1r.at[j], other_core)

    def send_2(j):
        return remote(s1_v.at[j, 1 - y], r2_v.at[j], s2s.at[j], s2r.at[j], other_y)

    def send_3(j, m):
        return remote(
            s2_v.at[j, flip(z, m, nz)], r3_v.at[j, m - 1], s3s.at[j, m], s3r.at[j, m], z_peer(m)
        )

    half = blocks * rows // 2
    quarter = half // 2
    home = home_v[...]
    row_id = lax.broadcasted_iota(jnp.int32, (rows, 1), 0)

    def step(j, carry):
        @pl.when(j < out_count)
        def _():
            for copy in dn_copies(j):
                copy.wait()
            slot = lax.rem(chunks + lax.div(j, per_slot), SLOTS)
            cols = pl.ds(pl.multiple_of(lax.rem(j, per_slot) * OUT_COLS, OUT_COLS), OUT_COLS)
            value = jnp.dot(
                hid_v[:, :GAT_COLS], w_v[slot, 0, :, cols], preferred_element_type=jnp.float32
            )
            value += jnp.dot(
                hid_v[:, GAT_COLS:], w_v[slot, 1, :, cols], preferred_element_type=jnp.float32
            )
            value = (value * share_v[:, :1]).astype(jnp.bfloat16)
            p_v[j, 0] = value[:half]
            p_v[j, 1] = value[half:]
            send_1(j).start()

        @pl.when((j >= LAG_1) & (j < out_count + LAG_1))
        def _():
            i = j - LAG_1
            send_1(i).wait_recv()
            value = p_v[i, core].astype(jnp.float32) + r1_v[i].astype(jnp.float32)
            value = value.astype(jnp.bfloat16)
            s1_v[i, 0] = value[:quarter]
            s1_v[i, 1] = value[quarter:]
            send_2(i).start()

        @pl.when((j >= LAG_2) & (j < out_count + LAG_2))
        def _():
            i = j - LAG_2
            send_2(i).wait_recv()
            value = s1_v[i, y].astype(jnp.float32) + r2_v[i].astype(jnp.float32)
            s2_v[i] = value.reshape(nz, rows, OUT_COLS).astype(jnp.bfloat16)
            for m in z_order:
                send_3(i, m).start()

        @pl.when(j >= LAG_3)
        def _():
            i = j - LAG_3
            value = s2_v[i, z].astype(jnp.float32)
            for m in z_order:
                send_3(i, m).wait_recv()
            for m in z_order:
                value += r3_v[i, m - 1].astype(jnp.float32)
            moved = jnp.zeros_like(value)
            for t in range(rows):
                moved = jnp.where(row_id == home[:, t : t + 1], value[t : t + 1, :], moved)
            cols = pl.ds(pl.multiple_of(i * OUT_COLS, OUT_COLS), OUT_COLS)
            out_ref[:, cols] = moved.astype(jnp.bfloat16)

        return carry

    lax.fori_loop(0, out_count + LAG_3, step, 0)

    send_own_y().wait_send()

    def drain_gather(g, carry):
        for m in range(1, nz):
            send_z(g, m).wait_send()
            send_y(g, m).wait_send()
        send_c(g).wait_send()
        return carry

    lax.fori_loop(0, chunks, drain_gather, 0)
    for m in z_order:
        table_z(m).wait_send()
    table_y().wait_send()
    table_c().wait_send()

    def drain(j, carry):
        send_1(j).wait_send()
        send_2(j).wait_send()
        for m in z_order:
            send_3(j, m).wait_send()
        return carry

    lax.fori_loop(0, out_count, drain, 0)


def fits_kernel(tokens, experts, bias, w_gate, device_count):
    rows, depth = tokens.shape
    ff = w_gate.shape[1]
    nz = device_count // 4
    return (
        device_count == bias.shape[0]
        and device_count == 4 * nz
        and nz & (nz - 1) == 0
        and nz > 1
        and rows == 8
        and 4 * bias.shape[0] <= LANES
        and depth % GAT_COLS == 0
        and depth % OUT_COLS == 0
        and ff == 2 * GAT_COLS
        and ff % HID_COLS == 0
        and ff % OUT_COLS == 0
        and depth // GAT_COLS >= SLOTS
        and -(-depth // ff) <= SLOTS
        and SLOTS * 4 * ff * GAT_COLS
        + 8 * device_count * rows * ff
        + 11 * device_count * rows * depth // 2
        < 66000000
    )


def per_device(tokens, experts, gate_fixed, home_slot, bias, w_gate, w_up, w_down):
    device_count = lax.axis_size("ep")
    if not fits_kernel(tokens, experts, bias, w_gate, device_count):
        return general(tokens, experts, gate_fixed, home_slot, bias, w_gate, w_up, w_down)
    rows, depth = tokens.shape
    top = experts.shape[1]
    ff = w_gate.shape[1]
    expert_count = bias.shape[0]
    nz = device_count // 4
    total = device_count * rows
    chunks = depth // GAT_COLS
    out_count = depth // OUT_COLS
    average = rows * device_count * top / expert_count
    bf16 = jnp.bfloat16
    dma = pltpu.SemaphoreType.DMA
    anywhere = pl.BlockSpec(memory_space=pl.ANY)
    out, bias_next = pl.pallas_call(
        functools.partial(moe_kernel, nz, expert_count, average),
        out_shape=(
            jax.ShapeDtypeStruct((rows, depth), bf16),
            jax.ShapeDtypeStruct((1, expert_count), jnp.float32),
        ),
        in_specs=[anywhere] * 8,
        out_specs=(
            pl.BlockSpec(memory_space=pltpu.VMEM),
            pl.BlockSpec(memory_space=pltpu.VMEM),
        ),
        scratch_shapes=[
            pltpu.VMEM((rows, top), jnp.int32),
            pltpu.VMEM((rows, top), jnp.int32),
            pltpu.VMEM((1, rows), jnp.int32),
            pltpu.VMEM((1, expert_count), jnp.float32),
            pltpu.VMEM((device_count, rows, depth), bf16),
            pltpu.VMEM((device_count, rows, LANES), bf16),
            pltpu.VMEM((total, GAT_COLS), bf16),
            pltpu.VMEM((SLOTS, 2, GAT_COLS, ff), bf16),
            pltpu.VMEM((2, total, ff), jnp.float32),
            pltpu.VMEM((total, ff), bf16),
            pltpu.VMEM((total, LANES), jnp.float32),
            pltpu.VMEM((out_count, 2, total // 2, OUT_COLS), bf16),
            pltpu.VMEM((out_count, total // 2, OUT_COLS), bf16),
            pltpu.VMEM((out_count, 2, total // 4, OUT_COLS), bf16),
            pltpu.VMEM((out_count, total // 4, OUT_COLS), bf16),
            pltpu.VMEM((out_count, nz, rows, OUT_COLS), bf16),
            pltpu.VMEM((out_count, nz - 1, rows, OUT_COLS), bf16),
            dma((5,)),
            dma((chunks, 2)),
            dma((out_count, 2)),
            dma((chunks + 1, nz)),
            dma((chunks + 1, nz)),
            dma((chunks + 1, nz)),
            dma((chunks + 1, nz)),
            dma((chunks + 1,)),
            dma((chunks + 1,)),
            dma((out_count,)),
            dma((out_count,)),
            dma((out_count,)),
            dma((out_count,)),
            dma((out_count, nz)),
            dma((out_count, nz)),
        ],
        compiler_params=pltpu.CompilerParams(
            collective_id=0, has_side_effects=True, vmem_limit_bytes=67043328
        ),
    )(
        tokens,
        experts,
        gate_fixed,
        home_slot.reshape(1, rows),
        bias.reshape(1, expert_count),
        w_gate,
        w_up,
        w_down,
    )
    return out, bias_next.reshape(expert_count)


def solution(mesh):
    placed = (
        P(("groups", "ep"), None),
        P(("groups", "ep"), None),
        P(("groups", "ep"), None),
        P(("groups", "ep")),
        P(),
        P(None, "ep"),
        P(None, "ep"),
        P("ep", None),
    )
    return jax.shard_map(
        per_device,
        mesh=mesh,
        in_specs=placed,
        out_specs=(P(("groups", "ep"), None), P("groups")),
        check_vma=False,
    )
```

time: 62.7 us -> 57.8 us (0.922)
  Pallas kernels: 59.3 us -> 54.3 us
    pallas_call x1, Pallas kernels: 59.3 us -> 54.3 us  [per_device(): pl.pallas_call(functools.partial(moe_kernel, nz, expert_count, average),...]
where the time goes in v1:
time: 57.8 us; the launch traced here: 57.6 us
  Pallas kernels  54.3 us (94%)
  local copies, waits for them, and re-layouts  2.66 us (5%)
  between operations  0.64 us (1%)
    pallas_call x1, Pallas kernels, per_device(): pl.pallas_call(functools.partial(moe_kernel, nz, expert_count, average),...  54.3 us
    unnamed x2, local copies, waits for them, and re-layouts  2.66 us

profile of v1, /device:TPU:0, one launch (start us, length us, event | category | flops | bytes accessed | tf_op | source)
XLA Modules:
  0.0 57.6 jit_solution(2680922548088856477)
XLA Ops:
  0.6 54.3 %shard_map.95 = (bf16[8,7168]{1,0:T(8,128)(2,1)}, f32[1,16]{1,0:T(1,128)}) custom-call(bf16[8,7168]{1,0:T(8,128)(2,1)} %tokens_hbm.1, s32[8,8]{1,0:T(8,128)} %experts_hbm.1, s32[8,8]{1,0:T(8,128)} %gates_hbm.1, s32[1,8]{1,0:T(1,128)} %bitcast.3, f32[1,16]{1,0:T(1,128)} %bitcast.4, bf16[7168,2048]{1,0:T(8,128)(2,1)} %wg_hbm.1, bf16[7168,2048]{1,0:T(8,128)(2,1)} %wu_hbm.1, ...), custom_call_target="tpu_custom_call" | custom-call | tf_op jit(solution)/shard_map/pallas_call | solution.py:510
  55.0 1.6 %copy.12 = bf16[8,7168]{1,0:T(8,128)(2,1)} copy(bf16[8,7168]{1,0:T(8,128)(2,1)} %get-tuple-element.8) | data formatting | bytes 229376
  56.5 1.1 %copy.13 = f32[16]{0:T(128)} copy(f32[16]{0:T(128)} %bitcast.5) | data formatting | bytes 128

commit v2 on v1

--- a/solution.py
+++ b/solution.py
@@ -85,11 +85,12 @@
 
 LANES = 128
 GAT_COLS = 1024
-OUT_COLS = 512
-HID_COLS = 1024
+OUT_COLS = 1024
+HID_COLS = 2048
 SLOTS = 6
 LAG_Y, LAG_C = 2, 3
-LAG_1, LAG_2, LAG_3 = 2, 6, 12
+WINDOW = 4
+LAG_1, LAG_2, LAG_3 = 1, 4, 7
 
 
 def flip(z, m, nz):
@@ -107,8 +108,7 @@
     out_ref, bias_out,
     exp_v, gate_v, home_v, bias_v, gath, tab_v, x_v, w_v, acc_v, hid_v, share_v,
     p_v, r1_v, s1_v, r2_v, s2_v, r3_v,
-    in_sem, gu_sem, dn_sem, zs, zr, ys, yr, cs, cr,
-    s1s, s1r, s2s, s2r, s3s, s3r,
+    in_sem, gu_sem, dn_sem, sent, zr, yr, cr, s1r, s2r, s3r,
 ):
     rows, depth = tokens_hbm.shape
     top = exp_v.shape[1]
@@ -164,7 +164,7 @@
         slot = lax.rem(g, SLOTS)
         part = pl.ds(pl.multiple_of(g * GAT_COLS, GAT_COLS), GAT_COLS)
         return [
-            pltpu.make_async_copy(w.at[part, :], w_v.at[slot, k], gu_sem.at[g, k])
+            pltpu.make_async_copy(w.at[part, :], w_v.at[slot, k], gu_sem.at[g])
             for k, w in enumerate((wg_hbm, wu_hbm))
         ]
 
@@ -176,10 +176,20 @@
             pltpu.make_async_copy(
                 wd_hbm.at[pl.ds(k * GAT_COLS, GAT_COLS), src],
                 w_v.at[slot, k, :, dst],
-                dn_sem.at[j, k],
+                dn_sem.at[j],
             )
             for k in range(2)
         ]
+
+    def gu_wait(g):
+        ref = w_v.at[lax.rem(g, SLOTS)]
+        pltpu.make_async_copy(ref, ref, gu_sem.at[g]).wait()
+
+    def dn_wait(j):
+        slot = lax.rem(chunks + lax.div(j, per_slot), SLOTS)
+        cols = pl.ds(pl.multiple_of(lax.rem(j, per_slot) * OUT_COLS, OUT_COLS), OUT_COLS)
+        ref = w_v.at[slot, :, :, cols]
+        pltpu.make_async_copy(ref, ref, dn_sem.at[j]).wait()
 
     def start_gu(g, carry):
         for copy in gu_copies(g):
@@ -209,31 +219,43 @@
 
     def send_z(g, m):
         ref = gath.at[mine, :, cols_of(g)]
-        return remote(ref, ref, zs.at[g, m], zr.at[g, m], z_peer(m))
+        return remote(ref, ref, sent.at[0], zr.at[g], z_peer(m))
+
+    def all_z(g):
+        ref = gath.at[pl.ds(0, nz - 1), :, cols_of(g)]
+        return remote(ref, ref, sent.at[0], zr.at[g], other_y)
 
     def send_y(g, m):
         ref = gath.at[slot_of(flip(z, m, nz), y, core), :, cols_of(g)]
-        return remote(ref, ref, ys.at[g, m], yr.at[g, m], other_y)
+        return remote(ref, ref, sent.at[1], yr.at[g], other_y)
+
+    def all_y(g):
+        ref = gath.at[pl.ds(0, nz - 1), :, cols_of(g)]
+        return remote(ref, ref, sent.at[1], yr.at[g], other_y)
 
     def send_own_y():
         ref = gath.at[mine]
-        return remote(ref, ref, ys.at[0, 0], yr.at[0, 0], other_y)
+        return remote(ref, ref, sent.at[1], yr.at[chunks], other_y)
 
     def send_c(g):
         ref = gath.at[pl.ds(core * side, side), :, cols_of(g)]
-        return remote(ref, ref, cs.at[g], cr.at[g], other_core)
+        return remote(ref, ref, sent.at[2], cr.at[g], other_core)
 
     def table_z(m):
         ref = tab_v.at[mine]
-        return remote(ref, ref, zs.at[chunks, m], zr.at[chunks, m], z_peer(m))
+        return remote(ref, ref, sent.at[3], zr.at[chunks], z_peer(m))
+
+    def all_table_z():
+        ref = tab_v.at[pl.ds(0, nz - 1)]
+        return remote(ref, ref, sent.at[3], zr.at[chunks], other_y)
 
     def table_y():
         ref = tab_v.at[pl.ds(slot_of(0, y, core), nz)]
-        return remote(ref, ref, ys.at[chunks, 0], yr.at[chunks, 0], other_y)
+        return remote(ref, ref, sent.at[4], yr.at[chunks + 1], other_y)
 
     def table_c():
         ref = tab_v.at[pl.ds(core * side, side)]
-        return remote(ref, ref, cs.at[chunks], cr.at[chunks], other_core)
+        return remote(ref, ref, sent.at[5], cr.at[chunks], other_core)
 
     z_order = list(range(nz - 1, 0, -1))
 
@@ -247,7 +269,7 @@
             send_z(g, m).start()
         return carry
 
-    lax.fori_loop(0, chunks, first_sends, 0)
+    first_sends(0, 0)
 
     for copy in small:
         copy.wait()
@@ -275,6 +297,7 @@
     tab_v[mine] = packed.astype(jnp.bfloat16)
     for m in z_order:
         table_z(m).start()
+    lax.fori_loop(1, min(WINDOW, chunks), first_sends, 0)
     acc_v[...] = jnp.zeros_like(acc_v)
 
     def spread(b, g):
@@ -289,20 +312,22 @@
         return g
 
     def stage_z(g):
+        all_z(g).wait_recv()
         for m in range(1, nz):
-            send_z(g, m).wait_recv()
             send_y(g, m).start()
 
+        @pl.when(g + WINDOW < chunks)
+        def _():
+            first_sends(g + WINDOW, 0)
+
     def stage_y(g):
-        for m in range(1, nz):
-            send_y(g, m).wait_recv()
+        all_y(g).wait_recv()
         send_c(g).start()
 
     def stage_c(g):
         send_c(g).wait_recv()
         lax.fori_loop(0, blocks // 2, spread, g)
-        for copy in gu_copies(g):
-            copy.wait()
+        gu_wait(g)
 
     def products(g, n):
         slot = lax.rem(g, SLOTS)
@@ -317,15 +342,14 @@
         def _():
             stage_z(i)
 
-        @pl.when(i == 0)
-        def _():
-            for m in z_order:
-                table_z(m).wait_recv()
+        @pl.when(i == LAG_Y)
+        def _():
+            all_table_z().wait_recv()
             table_y().start()
-
-        @pl.when(i == LAG_Y)
-        def _():
             send_own_y().wait_recv()
+
+        @pl.when(i == LAG_C + 2)
+        def _():
             table_y().wait_recv()
             table_c().start()
 
@@ -350,6 +374,16 @@
         return carry
 
     lax.fori_loop(0, chunks + LAG_C - 1, gather_step, 0)
+
+    stage_c(chunks - 1)
+
+    def last_body(n, carry):
+        gate, up, cols = products(chunks - 1, n)
+        hid_v[:, cols] = (gate / (1.0 + jnp.exp(-gate)) * up).astype(jnp.bfloat16)
+        return carry
+
+    lax.fori_loop(0, ff // HID_COLS, last_body, 0)
+    refill(chunks - 1)
 
     table_c().wait_recv()
     tables = tab_v[...].astype(jnp.float32).reshape(blocks * rows, LANES)
@@ -360,26 +394,22 @@
     load = jnp.sum(tables, axis=0, keepdims=True)[:, :experts_total]
     bias_out[...] = bias_v[...] + 2.0 / math.sqrt(average) * (average - load)
 
-    stage_c(chunks - 1)
-
-    def last_body(n, carry):
-        gate, up, cols = products(chunks - 1, n)
-        hid_v[:, cols] = (gate / (1.0 + jnp.exp(-gate)) * up).astype(jnp.bfloat16)
-        return carry
-
-    lax.fori_loop(0, ff // HID_COLS, last_body, 0)
-    refill(chunks - 1)
-
     def send_1(j):
-        return remote(p_v.at[j, 1 - core], r1_v.at[j], s1s.at[j], s1r.at[j], other_core)
+        return remote(p_v.at[j, 1 - core], r1_v.at[j], sent.at[6], s1r.at[j], other_core)
 
     def send_2(j):
-        return remote(s1_v.at[j, 1 - y], r2_v.at[j], s2s.at[j], s2r.at[j], other_y)
+        return remote(s1_v.at[j, 1 - y], r2_v.at[j], sent.at[7], s2r.at[j], other_y)
 
     def send_3(j, m):
         return remote(
-            s2_v.at[j, flip(z, m, nz)], r3_v.at[j, m - 1], s3s.at[j, m], s3r.at[j, m], z_peer(m)
+            s2_v.at[j, flip(z, m, nz)], r3_v.at[j, m - 1], sent.at[8], s3r.at[j], z_peer(m)
         )
+
+    def all_3(j):
+        return remote(r3_v.at[j], r3_v.at[j], sent.at[8], s3r.at[j], other_y)
+
+    def all_sent(ref, k):
+        remote(ref, ref, sent.at[k], zr.at[0], other_y).wait_send()
 
     half = blocks * rows // 2
     quarter = half // 2
@@ -389,8 +419,7 @@
     def step(j, carry):
         @pl.when(j < out_count)
         def _():
-            for copy in dn_copies(j):
-                copy.wait()
+            dn_wait(j)
             slot = lax.rem(chunks + lax.div(j, per_slot), SLOTS)
             cols = pl.ds(pl.multiple_of(lax.rem(j, per_slot) * OUT_COLS, OUT_COLS), OUT_COLS)
             value = jnp.dot(
@@ -423,12 +452,25 @@
             for m in z_order:
                 send_3(i, m).start()
 
+        @pl.when(j == LAG_2 + 1)
+        def _():
+            for k, ref in enumerate(
+                (
+                    gath.at[pl.ds(0, nz - 1)],
+                    gath.at[pl.ds(0, nz)],
+                    gath.at[pl.ds(0, side)],
+                    tab_v.at[pl.ds(0, nz - 1)],
+                    tab_v.at[pl.ds(0, nz)],
+                    tab_v.at[pl.ds(0, side)],
+                )
+            ):
+                all_sent(ref, k)
+
         @pl.when(j >= LAG_3)
         def _():
             i = j - LAG_3
             value = s2_v[i, z].astype(jnp.float32)
-            for m in z_order:
-                send_3(i, m).wait_recv()
+            all_3(i).wait_recv()
             for m in z_order:
                 value += r3_v[i, m - 1].astype(jnp.float32)
             moved = jnp.zeros_like(value)
@@ -441,29 +483,14 @@
 
     lax.fori_loop(0, out_count + LAG_3, step, 0)
 
-    send_own_y().wait_send()
-
-    def drain_gather(g, carry):
-        for m in range(1, nz):
-            send_z(g, m).wait_send()
-            send_y(g, m).wait_send()
-        send_c(g).wait_send()
-        return carry
-
-    lax.fori_loop(0, chunks, drain_gather, 0)
-    for m in z_order:
-        table_z(m).wait_send()
-    table_y().wait_send()
-    table_c().wait_send()
-
-    def drain(j, carry):
-        send_1(j).wait_send()
-        send_2(j).wait_send()
-        for m in z_order:
-            send_3(j, m).wait_send()
-        return carry
-
-    lax.fori_loop(0, out_count, drain, 0)
+    all_sent(p_v.at[:, 0], 6)
+    all_sent(s1_v.at[:, 0], 7)
+    all_sent(s2_v.at[:, pl.ds(0, nz - 1)], 8)
+
+
+def hand_over(out_in, bias_in, out_ref, bias_ref):
+    out_ref[...] = out_in[...]
+    bias_ref[...] = bias_in[...]
 
 
 def fits_kernel(tokens, experts, bias, w_gate, device_count):
@@ -510,8 +537,8 @@
     out, bias_next = pl.pallas_call(
         functools.partial(moe_kernel, nz, expert_count, average),
         out_shape=(
-            jax.ShapeDtypeStruct((rows, depth), bf16),
-            jax.ShapeDtypeStruct((1, expert_count), jnp.float32),
+            pltpu.VMEM((rows, depth), bf16),
+            pltpu.VMEM((1, expert_count), jnp.float32),
         ),
         in_specs=[anywhere] * 8,
         out_specs=(
@@ -537,23 +564,18 @@
             pltpu.VMEM((out_count, nz, rows, OUT_COLS), bf16),
             pltpu.VMEM((out_count, nz - 1, rows, OUT_COLS), bf16),
             dma((5,)),
-            dma((chunks, 2)),
-            dma((out_count, 2)),
-            dma((chunks + 1, nz)),
-            dma((chunks + 1, nz)),
-            dma((chunks + 1, nz)),
-            dma((chunks + 1, nz)),
+            dma((chunks,)),
+            dma((out_count,)),
+            dma((9,)),
             dma((chunks + 1,)),
+            dma((chunks + 2,)),
             dma((chunks + 1,)),
             dma((out_count,)),
             dma((out_count,)),
             dma((out_count,)),
-            dma((out_count,)),
-            dma((out_count, nz)),
-            dma((out_count, nz)),
         ],
         compiler_params=pltpu.CompilerParams(
-            collective_id=0, has_side_effects=True, vmem_limit_bytes=67043328
+            collective_id=0, has_side_effects=True, vmem_limit_bytes=66000000
         ),
     )(
         tokens,
@@ -565,6 +587,17 @@
         w_up,
         w_down,
     )
+    vmem = pl.BlockSpec(memory_space=pltpu.VMEM)
+    out, bias_next = pl.pallas_call(
+        hand_over,
+        out_shape=(
+            jax.ShapeDtypeStruct((rows, depth), bf16),
+            jax.ShapeDtypeStruct((1, expert_count), jnp.float32),
+        ),
+        in_specs=[vmem, vmem],
+        out_specs=(vmem, vmem),
+        compiler_params=pltpu.CompilerParams(vmem_limit_bytes=1000000),
+    )(out, bias_next)
     return out, bias_next.reshape(expert_count)
 
 

time: 57.8 us -> 46.3 us (0.80)
  Pallas kernels: 54.3 us -> 45.5 us
  local copies, waits for them, and re-layouts: 2.66 us -> 0 us
    pallas_call x1, Pallas kernels: 54.3 us -> 44.9 us  [per_device(): pl.pallas_call(functools.partial(moe_kernel, nz, expert_count, average),...]
    unnamed x2 -> x0, local copies, waits for them, and re-layouts: 2.66 us -> none
    pallas_call x0 -> x1, Pallas kernels: none -> 0.66 us  [per_device(): pl.pallas_call(hand_over, out_shape=(jax.ShapeDtypeStruct((rows, depth),...]
where the time goes in v2:
time: 46.3 us; the launch traced here: 46.2 us
  Pallas kernels  45.5 us (98%)
  between operations  0.64 us (1%)
    pallas_call x1, Pallas kernels, per_device(): pl.pallas_call(functools.partial(moe_kernel, nz, expert_count, average),...  44.9 us

profile of v2, /device:TPU:0, one launch (start us, length us, event | category | flops | bytes accessed | tf_op | source)
XLA Modules:
  0.0 46.2 jit_solution(18115886626688746108)
XLA Ops:
  0.6 44.9 %shard_map.95 = (bf16[8,7168]{1,0:T(8,128)(2,1)S(1)}, f32[1,16]{1,0:T(1,128)S(1)}) custom-call(bf16[8,7168]{1,0:T(8,128)(2,1)} %tokens_hbm.1, s32[8,8]{1,0:T(8,128)} %experts_hbm.1, s32[8,8]{1,0:T(8,128)} %gates_hbm.1, s32[1,8]{1,0:T(1,128)} %bitcast.3, f32[1,16]{1,0:T(1,128)} %bitcast.4, bf16[7168,2048]{1,0:T(8,128)(2,1)} %wg_hbm.1, ...), custom_call_target="tpu_custom_call" | custom-call | tf_op jit(solution)/shard_map/pallas_call | solution.py:537
  45.5 0.7 %shard_map.96 = (bf16[8,7168]{1,0:T(8,128)(2,1)}, f32[1,16]{1,0:T(1,128)}) custom-call(bf16[8,7168]{1,0:T(8,128)(2,1)S(1)} %get-tuple-element.6.out_in, f32[1,16]{1,0:T(1,128)S(1)} %get-tuple-element.7.bias_in), custom_call_target="tpu_custom_call" | custom-call | tf_op jit(solution)/shard_map/pallas_call | solution.py:591

commit v3 on v2

--- a/solution.py
+++ b/solution.py
@@ -89,7 +89,7 @@
 HID_COLS = 2048
 SLOTS = 6
 LAG_Y, LAG_C = 2, 3
-WINDOW = 4
+AHEAD_0, AHEAD_1 = 7, 2
 LAG_1, LAG_2, LAG_3 = 1, 4, 7
 
 
@@ -297,7 +297,8 @@
     tab_v[mine] = packed.astype(jnp.bfloat16)
     for m in z_order:
         table_z(m).start()
-    lax.fori_loop(1, min(WINDOW, chunks), first_sends, 0)
+    ahead = AHEAD_0 + (AHEAD_1 - AHEAD_0) * core
+    lax.fori_loop(1, ahead, first_sends, 0)
     acc_v[...] = jnp.zeros_like(acc_v)
 
     def spread(b, g):
@@ -316,9 +317,9 @@
         for m in range(1, nz):
             send_y(g, m).start()
 
-        @pl.when(g + WINDOW < chunks)
-        def _():
-            first_sends(g + WINDOW, 0)
+        @pl.when(g + ahead < chunks)
+        def _():
+            first_sends(g + ahead, 0)
 
     def stage_y(g):
         all_y(g).wait_recv()

time: 46.3 us -> 44.5 us (0.961)
  Pallas kernels: 45.5 us -> 43.7 us
    pallas_call x1, Pallas kernels: 44.9 us -> 43 us  [per_device(): pl.pallas_call(functools.partial(moe_kernel, nz, expert_count, average),...]
where the time goes in v3:
time: 44.5 us; the launch traced here: 44.3 us
  Pallas kernels  43.7 us (98%)
  between operations  0.64 us (1%)
    pallas_call x1, Pallas kernels, per_device(): pl.pallas_call(functools.partial(moe_kernel, nz, expert_count, average),...  43 us

profile of v3, /device:TPU:0, one launch (start us, length us, event | category | flops | bytes accessed | tf_op | source)
XLA Modules:
  0.0 44.3 jit_solution(9183800092003851209)
XLA Ops:
  0.6 43.0 %shard_map.95 = (bf16[8,7168]{1,0:T(8,128)(2,1)S(1)}, f32[1,16]{1,0:T(1,128)S(1)}) custom-call(bf16[8,7168]{1,0:T(8,128)(2,1)} %tokens_hbm.1, s32[8,8]{1,0:T(8,128)} %experts_hbm.1, s32[8,8]{1,0:T(8,128)} %gates_hbm.1, s32[1,8]{1,0:T(1,128)} %bitcast.3, f32[1,16]{1,0:T(1,128)} %bitcast.4, bf16[7168,2048]{1,0:T(8,128)(2,1)} %wg_hbm.1, ...), custom_call_target="tpu_custom_call" | custom-call | tf_op jit(solution)/shard_map/pallas_call | solution.py:538
  43.7 0.7 %shard_map.96 = (bf16[8,7168]{1,0:T(8,128)(2,1)}, f32[1,16]{1,0:T(1,128)}) custom-call(bf16[8,7168]{1,0:T(8,128)(2,1)S(1)} %get-tuple-element.6.out_in, f32[1,16]{1,0:T(1,128)S(1)} %get-tuple-element.7.bias_in), custom_call_target="tpu_custom_call" | custom-call | tf_op jit(solution)/shard_map/pallas_call | solution.py:592

commit v4 on v3

--- a/solution.py
+++ b/solution.py
@@ -85,12 +85,12 @@
 
 LANES = 128
 GAT_COLS = 1024
-OUT_COLS = 1024
+OUT_COLS = 512
 HID_COLS = 2048
 SLOTS = 6
 LAG_Y, LAG_C = 2, 3
 AHEAD_0, AHEAD_1 = 7, 2
-LAG_1, LAG_2, LAG_3 = 1, 4, 7
+LAG_1, LAG_2, LAG_3 = 2, 7, 13
 
 
 def flip(z, m, nz):
@@ -227,35 +227,35 @@
 
     def send_y(g, m):
         ref = gath.at[slot_of(flip(z, m, nz), y, core), :, cols_of(g)]
-        return remote(ref, ref, sent.at[1], yr.at[g], other_y)
+        return remote(ref, ref, sent.at[0], yr.at[g], other_y)
 
     def all_y(g):
         ref = gath.at[pl.ds(0, nz - 1), :, cols_of(g)]
-        return remote(ref, ref, sent.at[1], yr.at[g], other_y)
+        return remote(ref, ref, sent.at[0], yr.at[g], other_y)
 
     def send_own_y():
         ref = gath.at[mine]
-        return remote(ref, ref, sent.at[1], yr.at[chunks], other_y)
+        return remote(ref, ref, sent.at[0], yr.at[chunks], other_y)
 
     def send_c(g):
         ref = gath.at[pl.ds(core * side, side), :, cols_of(g)]
-        return remote(ref, ref, sent.at[2], cr.at[g], other_core)
+        return remote(ref, ref, sent.at[0], cr.at[g], other_core)
 
     def table_z(m):
         ref = tab_v.at[mine]
-        return remote(ref, ref, sent.at[3], zr.at[chunks], z_peer(m))
+        return remote(ref, ref, sent.at[1], zr.at[chunks], z_peer(m))
 
     def all_table_z():
         ref = tab_v.at[pl.ds(0, nz - 1)]
-        return remote(ref, ref, sent.at[3], zr.at[chunks], other_y)
+        return remote(ref, ref, sent.at[1], zr.at[chunks], other_y)
 
     def table_y():
         ref = tab_v.at[pl.ds(slot_of(0, y, core), nz)]
-        return remote(ref, ref, sent.at[4], yr.at[chunks + 1], other_y)
+        return remote(ref, ref, sent.at[1], yr.at[chunks + 1], other_y)
 
     def table_c():
         ref = tab_v.at[pl.ds(core * side, side)]
-        return remote(ref, ref, sent.at[5], cr.at[chunks], other_core)
+        return remote(ref, ref, sent.at[1], cr.at[chunks], other_core)
 
     z_order = list(range(nz - 1, 0, -1))
 
@@ -396,18 +396,18 @@
     bias_out[...] = bias_v[...] + 2.0 / math.sqrt(average) * (average - load)
 
     def send_1(j):
-        return remote(p_v.at[j, 1 - core], r1_v.at[j], sent.at[6], s1r.at[j], other_core)
+        return remote(p_v.at[j, 1 - core], r1_v.at[j], sent.at[2], s1r.at[j], other_core)
 
     def send_2(j):
-        return remote(s1_v.at[j, 1 - y], r2_v.at[j], sent.at[7], s2r.at[j], other_y)
+        return remote(s1_v.at[j, 1 - y], r2_v.at[j], sent.at[3], s2r.at[j], other_y)
 
     def send_3(j, m):
         return remote(
-            s2_v.at[j, flip(z, m, nz)], r3_v.at[j, m - 1], sent.at[8], s3r.at[j], z_peer(m)
+            s2_v.at[j, flip(z, m, nz)], r3_v.at[j, m - 1], sent.at[4], s3r.at[j], z_peer(m)
         )
 
     def all_3(j):
-        return remote(r3_v.at[j], r3_v.at[j], sent.at[8], s3r.at[j], other_y)
+        return remote(r3_v.at[j], r3_v.at[j], sent.at[4], s3r.at[j], other_y)
 
     def all_sent(ref, k):
         remote(ref, ref, sent.at[k], zr.at[0], other_y).wait_send()
@@ -455,17 +455,8 @@
 
         @pl.when(j == LAG_2 + 1)
         def _():
-            for k, ref in enumerate(
-                (
-                    gath.at[pl.ds(0, nz - 1)],
-                    gath.at[pl.ds(0, nz)],
-                    gath.at[pl.ds(0, side)],
-                    tab_v.at[pl.ds(0, nz - 1)],
-                    tab_v.at[pl.ds(0, nz)],
-                    tab_v.at[pl.ds(0, side)],
-                )
-            ):
-                all_sent(ref, k)
+            all_sent(gath.at[pl.ds(0, blocks - 1)], 0)
+            all_sent(tab_v.at[pl.ds(0, blocks - 1)], 1)
 
         @pl.when(j >= LAG_3)
         def _():
@@ -484,14 +475,20 @@
 
     lax.fori_loop(0, out_count + LAG_3, step, 0)
 
-    all_sent(p_v.at[:, 0], 6)
-    all_sent(s1_v.at[:, 0], 7)
-    all_sent(s2_v.at[:, pl.ds(0, nz - 1)], 8)
-
-
-def hand_over(out_in, bias_in, out_ref, bias_ref):
-    out_ref[...] = out_in[...]
-    bias_ref[...] = bias_in[...]
+    all_sent(p_v.at[:, 0], 2)
+    all_sent(s1_v.at[:, 0], 3)
+    all_sent(s2_v.at[:, pl.ds(0, nz - 1)], 4)
+
+
+def hand_over(out_in, bias_in, out_ref, bias_ref, sem):
+    copies = [
+        pltpu.make_async_copy(out_in, out_ref, sem.at[0]),
+        pltpu.make_async_copy(bias_in, bias_ref, sem.at[1]),
+    ]
+    for copy in copies:
+        copy.start()
+    for copy in copies:
+        copy.wait()
 
 
 def fits_kernel(tokens, experts, bias, w_gate, device_count):
@@ -567,7 +564,7 @@
             dma((5,)),
             dma((chunks,)),
             dma((out_count,)),
-            dma((9,)),
+            dma((5,)),
             dma((chunks + 1,)),
             dma((chunks + 2,)),
             dma((chunks + 1,)),
@@ -596,7 +593,8 @@
             jax.ShapeDtypeStruct((1, expert_count), jnp.float32),
         ),
         in_specs=[vmem, vmem],
-        out_specs=(vmem, vmem),
+        out_specs=(anywhere, anywhere),
+        scratch_shapes=[dma((2,))],
         compiler_params=pltpu.CompilerParams(vmem_limit_bytes=1000000),
     )(out, bias_next)
     return out, bias_next.reshape(expert_count)

time: 44.5 us -> 44.4 us (level)
  no operation moved by 1% of the time
where the time goes in v4:
time: 44.4 us; the launch traced here: 44.2 us
  Pallas kernels  43.6 us (98%)
  between operations  0.64 us (1%)
    pallas_call x1, Pallas kernels, per_device(): pl.pallas_call(functools.partial(moe_kernel, nz, expert_count, average),...  42.9 us

profile of v4, /device:TPU:0, one launch (start us, length us, event | category | flops | bytes accessed | tf_op | source)
XLA Modules:
  0.0 44.2 jit_solution(12407306802559425663)
XLA Ops:
  0.6 42.9 %shard_map.95 = (bf16[8,7168]{1,0:T(8,128)(2,1)S(1)}, f32[1,16]{1,0:T(1,128)S(1)}) custom-call(bf16[8,7168]{1,0:T(8,128)(2,1)} %tokens_hbm.1, s32[8,8]{1,0:T(8,128)} %experts_hbm.1, s32[8,8]{1,0:T(8,128)} %gates_hbm.1, s32[1,8]{1,0:T(1,128)} %bitcast.3, f32[1,16]{1,0:T(1,128)} %bitcast.4, bf16[7168,2048]{1,0:T(8,128)(2,1)} %wg_hbm.1, ...), custom_call_target="tpu_custom_call" | custom-call | tf_op jit(solution)/shard_map/pallas_call | solution.py:535
  43.5 0.7 %shard_map.96 = (bf16[8,7168]{1,0:T(8,128)(2,1)}, f32[1,16]{1,0:T(1,128)}) custom-call(bf16[8,7168]{1,0:T(8,128)(2,1)S(1)} %get-tuple-element.6.out_in, f32[1,16]{1,0:T(1,128)S(1)} %get-tuple-element.7.bias_in), custom_call_target="tpu_custom_call" | custom-call | tf_op jit(solution)/shard_map/pallas_call | solution.py:589
